TPU v7x, 32 devices: a whole 2x2x4 slice. The times are simulated.
32 devices in a mesh: prow: 8 (over z, y), pcol: 4 (over x, core).
Axes of the slice: x: 2, y: 2, z: 4, core: 2. Of those that a mesh axis runs over, the one named last changes fastest.
Arguments:
- iface_tiles: int32 [32, 16], replicated, may hold values from 0 to 63, as said below
- interior_sizes: int32 [32], P(('prow', 'pcol')), may hold values from 128 to 512
- coupling: float32 [32, 512, 2048], P(('prow', 'pcol')), may hold values from -0.25 to 0.25
- factor_inverse: float32 [32, 512, 512], P(('prow', 'pcol')), as said below
- interface_block: float32 [8, 8, 4, 16, 128, 128], P('prow', None, 'pcol'), as said below
Outputs:
- schur: float32 [8, 8, 4, 16, 128, 128], P('prow', None, 'pcol')
- panel: float32 [8, 8, 128, 128], P('prow', None, 'pcol')
Inputs may be any that keep to these rules, and one draw needn't show every extreme that they name: `iface_tiles`: each row holds 16 distinct tile numbers; for every r, exactly 2 of them are r modulo 8; every tile number stands in exactly 8 rows. `factor_inverse`: each matrix is lower triangular with a diagonal between 0.25 and 1. `interface_block`: diagonal entries lie between 80 and 160; other entries are of order one.
All inputs are finite; a program needn't handle non-finite values.
Results may differ from a plain program's by a relative error of at most 0.0001.
Values sent between devices are 32-bit elements; how exact they have to be, the bound alone decides.
A program may use at most 128 MiB of HBM per device.

v0:
```python
import jax
import jax.numpy as jnp
from jax import lax
from jax.sharding import PartitionSpec as P


def broadcast(block, axis, owner):
    block = jnp.where(lax.axis_index(axis) == owner, block, jnp.zeros_like(block))
    return lax.psum(block, axis)


def solve_panel(diag_block, column):
    lower = jnp.linalg.cholesky(0.5 * (diag_block + diag_block.T))
    flat = column.reshape(-1, diag_block.shape[0])
    solved = jax.scipy.linalg.solve_triangular(lower, flat.T, lower=True)
    return solved.T.reshape(column.shape)


def shards(iface_tiles, interior_sizes, coupling, factor_inverse, interface_block):
    rows_grid = lax.axis_size("prow")
    cols_grid = lax.axis_size("pcol")
    prow_index = lax.axis_index("prow")
    pcol_index = lax.axis_index("pcol")
    self_index = prow_index * cols_grid + pcol_index
    domains = iface_tiles.shape[0]
    tile_count = iface_tiles.shape[1]
    tile_width = interface_block.shape[-1]
    local_rows = interface_block.shape[1]
    local_cols = interface_block.shape[3]
    rows_per = tile_count // rows_grid
    cols_per = tile_count // cols_grid
    share_rows = tile_width // cols_grid
    live_count = interior_sizes[0]
    own_coupling = coupling[0]
    own_factor = factor_inverse[0]
    interior = own_coupling.shape[0]
    interior_live = (lax.iota(jnp.int32, interior) < live_count)[:, None]
    masked = jnp.where(interior_live, own_coupling, 0.0)
    own_tiles = lax.dynamic_index_in_dim(iface_tiles, self_index, 0, keepdims=False)
    row_order = jnp.argsort(own_tiles % rows_grid, stable=True)
    col_order = jnp.argsort(own_tiles % cols_grid, stable=True)
    weighted = jnp.dot(
        own_factor, masked, precision=lax.Precision.HIGHEST, preferred_element_type=jnp.float32
    )
    weighted = jnp.where(interior_live, weighted, 0.0).reshape(interior, tile_count, tile_width)
    row_part = jnp.take(weighted, row_order, axis=1).reshape(
        interior, rows_grid, rows_per, tile_width
    )
    col_part = jnp.take(weighted, col_order, axis=1).reshape(
        interior, cols_grid, cols_per, tile_width
    )
    contribution = -jnp.einsum(
        "kprt,kqcu->pqrctu", row_part, col_part, precision=lax.Precision.HIGHEST
    )
    received = lax.all_to_all(
        contribution.reshape(rows_grid * cols_grid, rows_per, cols_per, tile_width, tile_width),
        ("prow", "pcol"),
        split_axis=0,
        concat_axis=0,
        tiled=True,
    )
    sorted_rows = jnp.take_along_axis(
        iface_tiles, jnp.argsort(iface_tiles % rows_grid, axis=1, stable=True), axis=1
    )
    sorted_rows = sorted_rows.reshape(domains, rows_grid, rows_per)
    sorted_cols = jnp.take_along_axis(
        iface_tiles, jnp.argsort(iface_tiles % cols_grid, axis=1, stable=True), axis=1
    )
    sorted_cols = sorted_cols.reshape(domains, cols_grid, cols_per)
    target_rows = lax.dynamic_index_in_dim(sorted_rows, prow_index, 1, keepdims=False) // rows_grid
    target_cols = lax.dynamic_index_in_dim(sorted_cols, pcol_index, 1, keepdims=False) // cols_grid
    slot_ids = (target_rows[:, :, None] * local_cols + target_cols[:, None, :]).reshape(-1)
    base_tiles = interface_block.reshape(local_rows * local_cols, tile_width, tile_width)
    summed = base_tiles.at[slot_ids].add(received.reshape(-1, tile_width, tile_width))
    schur = summed.reshape(interface_block.shape)
    column = summed.reshape(local_rows, local_cols, tile_width, tile_width)[:, 0]
    diag_block = broadcast(column[0], "prow", 0)
    factored = solve_panel(diag_block, column)
    panel = broadcast(factored, "pcol", 0)
    own_share = lax.dynamic_slice_in_dim(panel, pcol_index * share_rows, share_rows, 1)
    return (schur, own_share[None])


def solution(mesh):
    in_specs = (
        P(),
        P(("prow", "pcol")),
        P(("prow", "pcol"), None, None),
        P(("prow", "pcol"), None, None),
        P("prow", None, "pcol", None, None, None),
    )
    out_specs = (P("prow", None, "pcol", None, None, None), P("prow", None, "pcol", None))
    return jax.shard_map(shards, mesh=mesh, in_specs=in_specs, out_specs=out_specs, check_vma=False)
```

profile of v0, /device:TPU:0, one launch (start us, length us, event | category | flops | bytes accessed | tf_op | source)
XLA Modules:
  0.0 673.2 jit_solution(10466884502546801936)
XLA Ops:
  7.2 8.0 %copy.40 = f32[1,8,1,16,128,128]{5,4,3,2,1,0:T(8,128)} copy(f32[1,8,1,16,128,128]{5,4,3,2,1,0:T(8,128)} %param.13) | data formatting | bytes 16777216
  15.2 0.2 dynamic-slice_reduce_fusion
  15.4 1.2 sort.64
  16.6 1.2 sort.65
  18.6 16.4 %fusion.3 = f32[2048,512]{1,0:T(8,128)} fusion(f32[1,512,2048]{2,1,0:T(8,128)} %param.11, pred[512]{0:T(512)(128)(4,1)S(1)} %iota_compare_fusion.2, f32[1,512,512]{2,1,0:T(8,128)S(1)} %copy-done), kind=kOutput, calls=%fused_computation.9 | convolution fusion | flops 6444548096 | bytes 9437696 | tf_op jit(solution)/shard_map/dot_general | solution.py:42
  35.0 5.0 gather_fusion.2
  40.0 5.0 gather_fusion.3
  44.9 2.9 broadcast_select_fusion.1
  47.9 0.5 copy-done.3
  48.4 0.6 broadcast_select_fusion
  49.0 30.0 %negate_bitcast_fusion = f32[8,4,2,4,128,128]{4,5,2,0,3,1:T(8,128)} fusion(f32[512,4,4,128,1,1]{0,3,5,4,2,1:T(8,128)S(1)} %bitcast.89, f32[512,8,2,128,1,1]{0,3,2,1,5,4:T(8,128)S(1)} %bitcast.90), kind=kOutput, calls=%fused_computation.5 | convolution fusion | flops 25773998080 | bytes 25165824 | tf_op jit(solution)/shard_map/kprt,kqcu->pqrctu/dot_general | solution.py:52
  79.0 17.4 %copy.23 = f32[8,4,2,4,128,128]{5,4,3,2,1,0:T(8,128)} copy(f32[8,4,2,4,128,128]{4,5,2,0,3,1:T(8,128)} %negate_bitcast_fusion) | data formatting | bytes 33554432 | tf_op jit(solution)/shard_map/neg | solution.py:52
  96.4 7.5 %all-to-all-start = ((f32[32,2,4,128,128]{4,3,2,1,0:T(8,128)}), f32[32,2,4,128,128]{4,3,2,1,0:T(8,128)}, u32[]{:S(2)}, u32[]{:S(2)}) async-start(f32[32,2,4,128,128]{4,3,2,1,0:T(8,128)} %bitcast.86), calls=%async_computation | async-start | bytes 33554432 | tf_op jit(solution)/shard_map/all_to_all | solution.py:55
  103.9 0.7 sort.63
  104.8 3.9 gather_fusion.1
  109.0 0.7 sort.62
  109.9 3.9 gather_fusion
  114.3 362.2 %all-to-all-done = f32[32,2,4,128,128]{4,3,2,1,0:T(8,128)} async-done(((f32[32,2,4,128,128]{4,3,2,1,0:T(8,128)}), f32[32,2,4,128,128]{4,3,2,1,0:T(8,128)}, u32[]{:S(2)}, u32[]{:S(2)}) %all-to-all-start) | async-done | bytes 16777248 | tf_op jit(solution)/shard_map/all_to_all | solution.py:55
  476.4 51.2 %scatter_fusion = f32[128,128,128]{2,1,0:T(8,128)} fusion(f32[128,128,128]{2,1,0:T(8,128)} %bitcast.84, s32[256]{0:T(256)S(1)} %bitcast.95, f32[256,128,128]{2,1,0:T(8,128)} %bitcast.24), kind=kCustom, calls=%fused_computation.4 | custom fusion | flops 4194304 | bytes 50332672 | tf_op jit(solution)/shard_map/scatter-add | solution.py:74
  527.7 9.1 %copy.24 = f32[128,128,128]{1,2,0:T(8,128)} copy(f32[128,128,128]{2,1,0:T(8,128)} %scatter_fusion) | data formatting | bytes 16777216 | tf_op jit(solution)/shard_map/scatter-add | solution.py:74
  536.7 1.5 fusion.10
  538.2 0.3 all-reduce.5.cloned.1.call-start
  538.5 65.0 %all-reduce.3.cloned.1.call-done = f32[128,128]{0,1:T(8,128)} async-done(((f32[128,128]{0,1:T(8,128)}), f32[128,128]{0,1:T(8,128)}) %all-reduce.3.cloned.1.call-update) | async-done | bytes 65552 | tf_op jit(solution)/shard_map/psum | solution.py:9
  603.5 0.9 copy.25
  604.5 0.9 fusion.13
  605.4 11.7 %cholesky.15 = f32[128,128]{1,0:T(8,128)S(1)} custom-call(f32[128,128]{1,0:T(8,128)S(1)} %fusion.12), custom_call_target="Cholesky" | custom-call | tf_op jit(solution)/shard_map/jit(cholesky)/cholesky | solution.py:13
  617.2 0.6 compare_reduce_fusion
  617.8 0.7 fusion.9
  618.5 9.8 %custom-call.7 = f32[1,128,128]{1,2,0:T(8,128)S(1)} custom-call(f32[1,128,128]{2,1,0:T(8,128)S(1)} %fusion.9), custom_call_target="InvertDiagBlocksLowerTriangular" | custom-call | tf_op jit(solution)/shard_map/jit(_solve_triangular)/triangular_solve | solution.py:15
  628.3 2.9 convolution_select_fusion
  631.2 33.5 %all-reduce.5.cloned.1.call-done = f32[8,128,128]{2,1,0:T(8,128)} async-done(((f32[8,128,128]{2,1,0:T(8,128)}), f32[8,128,128]{2,1,0:T(8,128)}) %all-reduce.5.cloned.1.call-update) | async-done | bytes 524304 | tf_op jit(solution)/shard_map/psum | solution.py:9
  664.7 1.6 dynamic-slice_bitcast_fusion
  (43 shorter events, 1.4 us)
Async XLA Ops:
  7.2 11.4 %copy-start = (f32[1,512,512]{2,1,0:T(8,128)S(1)}, f32[1,512,512]{2,1,0:T(8,128)}, u32[]{:S(2)}) copy-start(f32[1,512,512]{2,1,0:T(8,128)} %param.12) | copy-start | bytes 3145732
  7.2 8.0 %copy-start.2 = (s32[32,16]{0,1:T(8,128)S(1)}, s32[32,16]{0,1:T(8,128)}, u32[]{:S(2)}) copy-start(s32[32,16]{0,1:T(8,128)} %param.9) | copy-start | bytes 6148
  44.9 3.4 copy-start.3
  96.4 380.1 %all-to-all-start = ((f32[32,2,4,128,128]{4,3,2,1,0:T(8,128)}), f32[32,2,4,128,128]{4,3,2,1,0:T(8,128)}, u32[]{:S(2)}, u32[]{:S(2)}) async-start(f32[32,2,4,128,128]{4,3,2,1,0:T(8,128)} %bitcast.86), calls=%async_computation | async-start | bytes 33554432 | tf_op jit(solution)/shard_map/all_to_all | solution.py:55
  103.9 499.7 %all-reduce.3.cloned.1.call-start = ((), (), s32[]{:S(2)}) async-start(), calls=%async_computation.1 | async-start | bytes 131072 | tf_op jit(solution)/shard_map/psum | solution.py:9
  527.7 138.7 %copy-start.1 = (f32[1,512,512]{2,1,0:T(8,128)S(1)}, f32[1,512,512]{2,1,0:T(8,128)}, u32[]{:S(2)}) copy-start(f32[1,512,512]{2,1,0:T(8,128)} %param.12) | copy-start | bytes 3145732
  538.2 126.5 %all-reduce.5.cloned.1.call-start = ((), (), s32[]{:S(2)}) async-start(), calls=%async_computation.2 | async-start | bytes 1048576 | tf_op jit(solution)/shard_map/psum | solution.py:9
Sparse Core Ops, SparseCore 0:
  538.4 65.1 all-reduce.2
  631.4 33.3 all-reduce.4
where the time goes:
time: 675 us; the launch traced here: 673 us
  waiting for transfers between devices  461 us (68%)
  other arithmetic  84 us (12%)
  local copies, waits for them, and re-layouts  56.4 us (8%)
  matrix products  49.3 us (7%)
  between operations  14.9 us (2%)
  starting transfers between devices  7.76 us (1%)
    all_to_all x1, waiting for transfers between devices, shards(): lax.all_to_all(contribution.reshape(rows_grid * cols_grid, rows_per, cols...  362 us
    psum x2, waiting for transfers between devices, broadcast(): return lax.psum(block, axis)  98.5 us
    scatter-add x1, other arithmetic, shards(): base_tiles.at[slot_ids].add(received.reshape(-1, tile_width, tile_width))  51.2 us
    dot_general x1, matrix products, shards(): jnp.einsum('kprt,kqcu->pqrctu', row_part, col_part, precision=lax.Precisi...  30 us
    neg x1, local copies, waits for them, and re-layouts, shards(): -jnp.einsum('kprt,kqcu->pqrctu', row_part, col_part, precision=lax.Precis...  17.4 us
    dot_general x1, matrix products, shards(): jnp.dot(own_factor, masked, precision=lax.Precision.HIGHEST, preferred_el...  16.4 us
  transfers between devices with their start and end apart: 3, of which 3 were waited for; matrix products, arithmetic and copies ran while one was open for 2% of the time, Pallas kernels for 0%

commit v1 on v0

--- a/solution.py
+++ b/solution.py
@@ -6,7 +6,7 @@
 
 def broadcast(block, axis, owner):
     block = jnp.where(lax.axis_index(axis) == owner, block, jnp.zeros_like(block))
-    return lax.psum(block, axis)
+    return jnp.sum(lax.all_gather(block, axis), axis=0)
 
 
 def solve_panel(diag_block, column):

time: 675 us -> 615 us (0.911)
  waiting for transfers between devices: 461 us -> 381 us
  blocking collectives: 0 us -> 31.6 us
  local copies, waits for them, and re-layouts: 56.4 us -> 45.5 us
    psum x2 -> x0, waiting for transfers between devices: 98.5 us -> none  [broadcast(): return lax.psum(block, axis)]
    all_gather x0 -> x1, blocking collectives: none -> 31.6 us  [broadcast(): return jnp.sum(lax.all_gather(block, axis), axis=0)]
    all_gather x0 -> x1, waiting for transfers between devices: none -> 19 us  [broadcast(): return jnp.sum(lax.all_gather(block, axis), axis=0)]
    scatter-add x1 -> x0, local copies, waits for them, and re-layouts: 9.09 us -> none  [shards(): base_tiles.at[slot_ids].add(received.reshape(-1, tile_width, tile_width))]
  transfers between devices with their start and end apart: 3 -> 2, of which waited for: 3 -> 2; matrix products, arithmetic and copies ran while one was open for 2% -> 2% of each run, Pallas kernels for 0% -> 0%
where the time goes in v1:
time: 615 us; the launch traced here: 614 us
  waiting for transfers between devices  381 us (62%)
  other arithmetic  84.4 us (14%)
  matrix products  48.8 us (8%)
  local copies, waits for them, and re-layouts  45.5 us (7%)
  blocking collectives  31.6 us (5%)
  between operations  14.9 us (2%)
  starting transfers between devices  7.5 us (1%)
    all_to_all x1, waiting for transfers between devices, shards(): lax.all_to_all(contribution.reshape(rows_grid * cols_grid, rows_per, cols...  362 us
    scatter-add x1, other arithmetic, shards(): base_tiles.at[slot_ids].add(received.reshape(-1, tile_width, tile_width))  51.2 us
    all_gather x1, blocking collectives, broadcast(): return jnp.sum(lax.all_gather(block, axis), axis=0)  31.6 us
    dot_general x1, matrix products, shards(): jnp.einsum('kprt,kqcu->pqrctu', row_part, col_part, precision=lax.Precisi...  30 us
    all_gather x1, waiting for transfers between devices, broadcast(): return jnp.sum(lax.all_gather(block, axis), axis=0)  19 us
    neg x1, local copies, waits for them, and re-layouts, shards(): -jnp.einsum('kprt,kqcu->pqrctu', row_part, col_part, precision=lax.Precis...  17.4 us
    dot_general x1, matrix products, shards(): jnp.dot(own_factor, masked, precision=lax.Precision.HIGHEST, preferred_el...  16.4 us
    another operation x3, other arithmetic, solve_panel(): lower = jnp.linalg.cholesky(0.5 * (diag_block + diag_block.T))  12.4 us
  transfers between devices with their start and end apart: 2, of which 2 were waited for; matrix products, arithmetic and copies ran while one was open for 2% of the time, Pallas kernels for 0%

profile of v1, /device:TPU:0, one launch (start us, length us, event | category | flops | bytes accessed | tf_op | source)
XLA Modules:
  0.0 613.9 jit_solution(4093995834380125606)
XLA Ops:
  7.2 8.0 %copy.44 = f32[1,8,1,16,128,128]{5,4,3,2,1,0:T(8,128)} copy(f32[1,8,1,16,128,128]{5,4,3,2,1,0:T(8,128)} %param.13) | data formatting | bytes 16777216
  15.2 0.2 dynamic-slice_reduce_fusion
  15.4 1.2 sort.64
  16.6 1.2 sort.65
  18.6 16.4 %fusion.3 = f32[2048,512]{1,0:T(8,128)} fusion(f32[1,512,2048]{2,1,0:T(8,128)} %param.11, pred[512]{0:T(512)(128)(4,1)S(1)} %iota_compare_fusion.2, f32[1,512,512]{2,1,0:T(8,128)S(1)} %copy-done), kind=kOutput, calls=%fused_computation.9 | convolution fusion | flops 6444548096 | bytes 9437696 | tf_op jit(solution)/shard_map/dot_general | solution.py:42
  35.0 5.0 gather_fusion.2
  40.0 5.0 gather_fusion.3
  44.9 2.9 broadcast_select_fusion.1
  47.9 0.5 copy-done.3
  48.4 0.6 broadcast_select_fusion
  49.0 30.0 %negate_bitcast_fusion = f32[8,4,2,4,128,128]{4,5,2,0,3,1:T(8,128)} fusion(f32[512,4,4,128,1,1]{0,3,5,4,2,1:T(8,128)S(1)} %bitcast.90, f32[512,8,2,128,1,1]{0,3,2,1,5,4:T(8,128)S(1)} %bitcast.91), kind=kOutput, calls=%fused_computation.5 | convolution fusion | flops 25773998080 | bytes 25165824 | tf_op jit(solution)/shard_map/kprt,kqcu->pqrctu/dot_general | solution.py:52
  79.0 17.4 %copy.31 = f32[8,4,2,4,128,128]{5,4,3,2,1,0:T(8,128)} copy(f32[8,4,2,4,128,128]{4,5,2,0,3,1:T(8,128)} %negate_bitcast_fusion) | data formatting | bytes 33554432 | tf_op jit(solution)/shard_map/neg | solution.py:52
  96.4 7.5 %all-to-all-start = ((f32[32,2,4,128,128]{4,3,2,1,0:T(8,128)}), f32[32,2,4,128,128]{4,3,2,1,0:T(8,128)}, u32[]{:S(2)}, u32[]{:S(2)}) async-start(f32[32,2,4,128,128]{4,3,2,1,0:T(8,128)} %bitcast.87), calls=%async_computation | async-start | bytes 33554432 | tf_op jit(solution)/shard_map/all_to_all | solution.py:55
  103.9 0.7 sort.63
  104.8 3.9 gather_fusion.1
  108.9 0.1 copy.29
  109.0 0.7 sort.62
  109.9 3.9 gather_fusion
  114.0 0.1 broadcast_add_fusion
  114.1 0.1 add.118
  114.3 362.2 %all-to-all-done = f32[32,2,4,128,128]{4,3,2,1,0:T(8,128)} async-done(((f32[32,2,4,128,128]{4,3,2,1,0:T(8,128)}), f32[32,2,4,128,128]{4,3,2,1,0:T(8,128)}, u32[]{:S(2)}, u32[]{:S(2)}) %all-to-all-start) | async-done | bytes 16777248 | tf_op jit(solution)/shard_map/all_to_all | solution.py:55
  476.4 51.2 %scatter_fusion = f32[128,128,128]{2,1,0:T(8,128)} fusion(f32[128,128,128]{2,1,0:T(8,128)} %bitcast.83, s32[256]{0:T(256)S(1)} %bitcast.95, f32[256,128,128]{2,1,0:T(8,128)} %bitcast.24), kind=kCustom, calls=%fused_computation.4 | custom fusion | flops 4194304 | bytes 50332672 | tf_op jit(solution)/shard_map/scatter-add | solution.py:74
  527.7 0.8 slice_select_fusion
  528.5 31.6 %all-gather = f32[8,1,128,128]{3,2,1,0:T(8,128)S(1)} all-gather(f32[1,1,128,128]{3,2,1,0:T(8,128)S(1)} %slice_select_fusion), channel_id=2, replica_groups=mesh['prow'=8,'pcol'=4] {'prow'}, dimensions={0}, use_global_device_ids=true | all-gather | bytes 589824 | tf_op jit(solution)/shard_map/all_gather | solution.py:9
  560.2 11.7 %cholesky.15 = f32[128,128]{1,0:T(8,128)S(1)} custom-call(f32[128,128]{1,0:T(8,128)S(1)} %fusion.12), custom_call_target="Cholesky" | custom-call | tf_op jit(solution)/shard_map/jit(cholesky)/cholesky | solution.py:13
  572.0 0.6 compare_reduce_fusion
  572.6 0.7 fusion.9
  573.3 9.8 %custom-call.7 = f32[1,128,128]{1,2,0:T(8,128)S(1)} custom-call(f32[1,128,128]{2,1,0:T(8,128)S(1)} %fusion.9), custom_call_target="InvertDiagBlocksLowerTriangular" | custom-call | tf_op jit(solution)/shard_map/jit(_solve_triangular)/triangular_solve | solution.py:15
  583.1 2.4 convolution_select_fusion
  585.5 19.0 %all-gather.4.cloned.1.call-done = f32[32,128,128]{2,1,0:T(8,128)} async-done(((f32[8,128,128]{2,1,0:T(8,128)}), f32[32,128,128]{2,1,0:T(8,128)}) %all-gather.4.cloned.1.call-update) | async-done | bytes 2097168 | tf_op jit(solution)/shard_map/all_gather | solution.py:9
  604.6 1.8 reduce_sum.19
  606.4 0.7 dynamic-slice_bitcast_fusion
  (40 shorter events, 1.1 us)
Async XLA Ops:
  7.2 11.4 %copy-start = (f32[1,512,512]{2,1,0:T(8,128)S(1)}, f32[1,512,512]{2,1,0:T(8,128)}, u32[]{:S(2)}) copy-start(f32[1,512,512]{2,1,0:T(8,128)} %param.12) | copy-start | bytes 3145732
  7.2 8.0 %copy-start.2 = (s32[32,16]{0,1:T(8,128)S(1)}, s32[32,16]{0,1:T(8,128)}, u32[]{:S(2)}) copy-start(s32[32,16]{0,1:T(8,128)} %param.9) | copy-start | bytes 6148
  44.9 3.4 copy-start.3
  96.4 380.1 %all-to-all-start = ((f32[32,2,4,128,128]{4,3,2,1,0:T(8,128)}), f32[32,2,4,128,128]{4,3,2,1,0:T(8,128)}, u32[]{:S(2)}, u32[]{:S(2)}) async-start(f32[32,2,4,128,128]{4,3,2,1,0:T(8,128)} %bitcast.87), calls=%async_computation | async-start | bytes 33554432 | tf_op jit(solution)/shard_map/all_to_all | solution.py:55
  103.9 500.7 %all-gather.4.cloned.1.call-start = ((), (), s32[]{:S(2)}) async-start(), calls=%async_computation.1 | async-start | bytes 2621440 | tf_op jit(solution)/shard_map/all_gather | solution.py:9
  476.4 130.6 %copy-start.1 = (f32[1,512,512]{2,1,0:T(8,128)S(1)}, f32[1,512,512]{2,1,0:T(8,128)}, u32[]{:S(2)}) copy-start(f32[1,512,512]{2,1,0:T(8,128)} %param.12) | copy-start | bytes 3145732
Sparse Core Ops, SparseCore 0:
  585.7 18.8 all-gather.3
